TPU v7x, 32 devices: a whole 2x2x4 slice. The times are simulated.
32 devices in a mesh: dp: 16 (over z, x, core), tensor: 2 (over y).
Axes of the slice: x: 2, y: 2, z: 4, core: 2. Of those that a mesh axis runs over, the one named last changes fastest.
Arguments:
- hidden: bfloat16 [5120, 18432], P('dp', 'tensor'), may hold values from -6 to 6
- fixed_down_weight: bfloat16 [18432, 4608], P('tensor', 'dp'), may hold values from -4 to 4
- lowrank_factor_b: bfloat16 [18432, 16], P('tensor'), may hold values from -0.046875 to 0.046875
- lowrank_factor_a: bfloat16 [16, 4608], P(None, 'dp'), may hold values from -1.5 to 1.5
- magnitude: float32 [4608], P('tensor'), may hold values from 0.5 to 2
- cotangent: bfloat16 [5120, 4608], P('dp', 'tensor'), may hold values from -0.083496094 to 0.083496094
Outputs:
- mixed: bfloat16 [5120, 4608], P('dp', 'tensor')
- gradient_column_scale: float32 [4608], P(('tensor', 'dp'))
- gradient_factor_a: float32 [16, 4608], P(None, ('tensor', 'dp'))
- gradient_factor_b: float32 [18432, 16], P(('tensor', 'dp'))
All inputs are finite; a program needn't handle non-finite values.
Results may differ from a plain program's by a relative error of at most 0.0054.
Values may be sent and summed in bfloat16 or wider, within the bound.
No kernel may reach another device: no remote copies, remote signals or barrier semaphores. Data moves between devices by JAX's collectives and lax.ppermute only.
A program may use at most 192 MiB of HBM per device.

v0:
```python
import jax
import jax.numpy as jnp
from jax import lax
from jax.sharding import PartitionSpec as P


def body(hidden, fixed_down_weight, lowrank_factor_b, lowrank_factor_a, magnitude, cotangent):
    out_cols = magnitude.shape[0]
    own = lax.axis_index("tensor")
    lowrank_portion = jnp.dot(hidden, lowrank_factor_b, preferred_element_type=jnp.float32)
    combined_weight = fixed_down_weight.astype(jnp.float32) + jnp.dot(
        lowrank_factor_b, lowrank_factor_a, preferred_element_type=jnp.float32
    )
    local_sq = jnp.sum(combined_weight * combined_weight, axis=0)
    low_full, block_sq = lax.psum((lowrank_portion, local_sq), "tensor")
    col_sq = lax.all_gather(block_sq, "dp", axis=0, tiled=True)
    sq_len = 1
    weight_shape = (1, 1)
    squares = jnp.zeros((sq_len,), jnp.float32)
    full_w = jnp.zeros(weight_shape, jnp.bfloat16)
    w_piece = lax.all_gather(fixed_down_weight, "dp", axis=1, tiled=True)
    factor_a_slice = lax.all_gather(lowrank_factor_a, "dp", axis=1, tiled=True)
    products = jnp.dot(hidden, w_piece, preferred_element_type=jnp.float32)
    full_a = factor_a_slice
    products, squares, full_a, full_w = (products, squares, full_a, full_w)
    column_norm_values = jnp.sqrt(col_sq + 1e-06)
    own_norms = lax.dynamic_slice_in_dim(column_norm_values, own * out_cols, out_cols, 0)
    scale = magnitude / own_norms
    lowrank_block_update = low_full.astype(jnp.bfloat16)
    summed = lax.psum_scatter(products, "tensor", scatter_dimension=1, tiled=True)
    own_a = lax.dynamic_slice_in_dim(full_a, own * out_cols, out_cols, 1)
    prenorm_output = summed + jnp.dot(
        lowrank_block_update, own_a, preferred_element_type=jnp.float32
    )
    mixed = (prenorm_output * scale).astype(jnp.bfloat16)
    cot = cotangent.astype(jnp.float32)
    mag_part = jnp.sum(cot * prenorm_output, axis=0) / own_norms
    prenorm_gradient_b = (cot * scale).astype(jnp.bfloat16)
    factor_a_portion = jnp.dot(
        lowrank_block_update.T, prenorm_gradient_b, preferred_element_type=jnp.float32
    )
    back_part = jnp.dot(prenorm_gradient_b, own_a.T, preferred_element_type=jnp.float32)
    backward_factor_b = lax.psum(back_part, "tensor").astype(jnp.bfloat16)
    b_part = jnp.dot(hidden.T, backward_factor_b, preferred_element_type=jnp.float32)
    gradient_column_scale, gradient_factor_b = (
        lax.psum_scatter(mag_part, "dp", scatter_dimension=0, tiled=True),
        lax.psum_scatter(b_part, "dp", scatter_dimension=0, tiled=True),
    )
    gradient_factor_a = lax.psum_scatter(factor_a_portion, "dp", scatter_dimension=1, tiled=True)
    return (mixed, gradient_column_scale, gradient_factor_a, gradient_factor_b)


def solution(mesh):
    return jax.shard_map(
        body,
        mesh=mesh,
        in_specs=(
            P("dp", "tensor"),
            P("tensor", "dp"),
            P("tensor", None),
            P(None, "dp"),
            P("tensor"),
            P("dp", "tensor"),
        ),
        out_specs=(
            P("dp", "tensor"),
            P(("tensor", "dp")),
            P(None, ("tensor", "dp")),
            P(("tensor", "dp"), None),
        ),
        check_vma=False,
    )
```

profile of v0, /device:TPU:0, one launch (start us, length us, event | category | flops | bytes accessed | tf_op | source)
XLA Modules:
  0.0 711.5 jit_solution(8600215113139559798)
XLA Ops:
  7.2 0.7 all-gather.3.cloned.1.call-update
  8.0 24.5 %all-gather = bf16[16,288,16]{1,2,0:T(8,128)(2,1)S(1)} all-gather(bf16[1,288,16]{1,2,0:T(8,128)(2,1)S(1)} %bitcast.24), channel_id=1, replica_groups=mesh['dp'=16,'tensor'=2] {'dp'}, dimensions={0}, use_global_device_ids=true | all-gather | bytes 156672 | tf_op jit(solution)/shard_map/all_gather | solution.py:22
  32.6 0.2 reshape.13
  32.8 0.6 fusion.17
  34.1 4.4 fusion.3
  38.4 4.9 psum.22
  43.4 0.2 dynamic-update-slice
  43.6 61.0 %all-reduce = f32[4608]{0:T(1024)S(1)} all-reduce(f32[4608]{0:T(1024)S(1)} %dynamic-update-slice), channel_id=1, replica_groups=mesh['dp'=16,'tensor'=2] {'dp'}, use_global_device_ids=true, to_apply=%add | all-reduce | flops 4608 | bytes 36864
  104.7 0.5 fusion.4
  105.2 4.3 fusion.19
  109.6 8.7 %all-reduce.2 = (bf16[320,16]{0,1:T(8,128)(2,1)S(1)}, bf16[320,16]{0,1:T(8,128)(2,1)S(1)}) all-reduce(f32[320,16]{0,1:T(8,128)S(1)} %fusion.19, f32[320,16]{0,1:T(8,128)S(1)} %fusion.4), channel_id=1, replica_groups=mesh['dp'=16,'tensor'=2] {'tensor'}, use_global_device_ids=true, to_apply=%region_1.0 | all-reduce | flops 10240 | bytes 61440 | tf_op jit(solution)/shard_map/psum | solution.py:15
  118.3 1.8 convolution_bitcast_fusion.1
  120.2 3.7 convolution_bitcast_fusion
  123.9 2.9 copy.14
  126.8 296.7 %all-gather.3.cloned.1.call-done = bf16[9216,4608]{0,1:T(8,128)(2,1)} async-done(((bf16[9216,288]{0,1:T(8,128)(2,1)}), bf16[9216,4608]{0,1:T(8,128)(2,1)}) %all-gather.3.cloned.1.call-update) | async-done | bytes 84934672 | tf_op jit(solution)/shard_map/all_gather | solution.py:21
  423.6 40.2 %fusion.18 = f32[320,4608]{1,0:T(8,128)} fusion(bf16[320,9216]{1,0:T(8,128)(2,1)} %param.6, bf16[9216,4608]{0,1:T(8,128)(2,1)} %all-gather.3.cloned.1.call-done), kind=kOutput, calls=%fused_computation.24 | convolution fusion | flops 27179089920 | bytes 96731136 | tf_op jit(solution)/shard_map/dot_general | solution.py:23
  464.4 22.3 %reduce-scatter.10.cloned.1.call-done = f32[144,16]{1,0:T(8,128)} async-done(((f32[2304,16]{1,0:T(8,128)}), f32[144,16]{1,0:T(8,128)}) %reduce-scatter.10.cloned.1.call-update) | async-done | bytes 9232
  486.7 1.6 copy.13
  488.3 77.0 %reduce-scatter.12.cloned.1.call-done = f32[576,16]{1,0:T(8,128)} async-done(((f32[9216,16]{1,0:T(8,128)}), f32[576,16]{1,0:T(8,128)}) %reduce-scatter.12.cloned.1.call-update) | async-done | bytes 36880
  565.2 1.7 copy.15
  566.9 72.6 %reduce-scatter.8.cloned.1.call-done = f32[320,2304]{1,0:T(8,128)} async-done(((f32[320,4608]{1,0:T(8,128)}), f32[320,2304]{1,0:T(8,128)}) %reduce-scatter.8.cloned.1.call-update) | async-done | bytes 2949136 | tf_op jit(solution)/shard_map/reduce_scatter | solution.py:30
  639.6 3.7 fusion.1
  643.3 61.0 %all-reduce.1 = f32[2304]{0:T(1024)S(1)} all-reduce(f32[2304]{0:T(1024)S(1)} %fusion.12), channel_id=3, replica_groups=mesh['dp'=16,'tensor'=2] {'dp'}, use_global_device_ids=true, to_apply=%region_5.0.clone | all-reduce | flops 2304 | bytes 18432
  704.4 0.6 dynamic-slice.3
  (21 shorter events, 0.5 us)
Async XLA Ops:
  7.2 26.9 %copy-start = (bf16[9216,16]{0,1:T(8,128)(2,1)S(1)}, bf16[9216,16]{0,1:T(8,128)(2,1)}, u32[]{:S(2)}) copy-start(bf16[9216,16]{0,1:T(8,128)(2,1)} %param.8) | copy-start | bytes 884740
  7.2 25.6 %copy-start.4 = (u32[32]{0:T(128)S(1)}, u32[32]{0:T(128)}, u32[]{:S(2)}) copy-start(u32[32]{0:T(128)} %constant.16) | copy-start | bytes 388
  7.2 0.8 copy-start.2
  7.2 416.4 %all-gather.3.cloned.1.call-start = ((), (), s32[]{:S(2)}) async-start(), calls=%async_computation.3 | async-start | bytes 90243072 | tf_op jit(solution)/shard_map/all_gather | solution.py:21
  7.9 478.8 %reduce-scatter.10.cloned.1.call-start = ((), (), s32[]{:S(2)}) async-start(), calls=%async_computation.5 | async-start | bytes 1253376
  34.0 70.6 %copy-start.3 = (f32[2304]{0:T(1024)S(1)}, f32[2304]{0:T(1024)}, u32[]{:S(2)}) copy-start(f32[2304]{0:T(1024)} %param.10) | copy-start | bytes 27652
  34.0 70.7 %copy-start.1 = (bf16[320,2304]{1,0:T(8,128)(2,1)S(1)}, bf16[320,2304]{1,0:T(8,128)(2,1)}, u32[]{:S(2)}) copy-start(bf16[320,2304]{1,0:T(8,128)(2,1)} %param.11) | copy-start | bytes 4423684
  120.1 445.1 %reduce-scatter.12.cloned.1.call-start = ((), (), s32[]{:S(2)}) async-start(), calls=%async_computation.6 | async-start | bytes 5013504
  126.8 512.8 %reduce-scatter.8.cloned.1.call-start = ((), (), s32[]{:S(2)}) async-start(), calls=%async_computation.4 | async-start | bytes 8847360 | tf_op jit(solution)/shard_map/reduce_scatter | solution.py:30
Sparse Core Ops, SparseCore 0:
  9.6 413.9 all-gather.2
  427.7 58.9 reduce-scatter.9
  490.6 74.6 reduce-scatter.11
  567.4 72.1 reduce-scatter.7
where the time goes:
time: 712 us
  waiting for transfers between devices  469 us (66%)
  blocking collectives  160 us (22%)
  matrix products  58.6 us (8%)
  between operations  15.2 us (2%)
  local copies, waits for them, and re-layouts  7.9 us (1%)
    all_gather x1, waiting for transfers between devices, body(): w_piece = lax.all_gather(fixed_down_weight, 'dp', axis=1, tiled=True)  297 us
    unnamed x2, blocking collectives  122 us
    unnamed x6, waiting for transfers between devices  100 us
    reduce_scatter x1, waiting for transfers between devices, body(): lax.psum_scatter(products, 'tensor', scatter_dimension=1, tiled=True)  72.6 us
    dot_general x1, matrix products, body(): products = jnp.dot(hidden, w_piece, preferred_element_type=jnp.float32)  40.2 us
    all_gather x1, blocking collectives, body(): factor_a_slice = lax.all_gather(lowrank_factor_a, 'dp', axis=1, tiled=True)  24.5 us
  transfers between devices with their start and end apart: 4, of which 4 were waited for; matrix products, arithmetic and copies ran while one was open for 9% of the time, Pallas kernels for 0%

commit v1 on v0

--- a/solution.py
+++ b/solution.py
@@ -2,6 +2,7 @@
 import jax.numpy as jnp
 from jax import lax
 from jax.sharding import PartitionSpec as P
+from jax.lax import all_gather
 
 
 def body(hidden, fixed_down_weight, lowrank_factor_b, lowrank_factor_a, magnitude, cotangent):
@@ -18,7 +19,7 @@
     weight_shape = (1, 1)
     squares = jnp.zeros((sq_len,), jnp.float32)
     full_w = jnp.zeros(weight_shape, jnp.bfloat16)
-    w_piece = lax.all_gather(fixed_down_weight, "dp", axis=1, tiled=True)
+    w_piece = jnp.concatenate(all_gather(fixed_down_weight, "dp"), axis=1)
     factor_a_slice = lax.all_gather(lowrank_factor_a, "dp", axis=1, tiled=True)
     products = jnp.dot(hidden, w_piece, preferred_element_type=jnp.float32)
     full_a = factor_a_slice

time: 712 us -> 721 us (1.013)
  local copies, waits for them, and re-layouts: 7.9 us -> 121 us
  waiting for transfers between devices: 469 us -> 368 us
    unnamed x6, waiting for transfers between devices: 100 us -> 0.75 us
    reshape x0 -> x1, local copies, waits for them, and re-layouts: none -> 56.8 us  [body(): w_piece = jnp.concatenate(all_gather(fixed_down_weight, 'dp'), axis=1)]
    unnamed x18 -> x41, local copies, waits for them, and re-layouts: 7.86 us -> 64.5 us
  transfers between devices with their start and end apart: 4 -> 4, of which waited for: 4 -> 2; matrix products, arithmetic and copies ran while one was open for 9% -> 24% of each run, Pallas kernels for 0% -> 0%
where the time goes in v1:
time: 721 us
  waiting for transfers between devices  368 us (51%)
  blocking collectives  160 us (22%)
  local copies, waits for them, and re-layouts  121 us (17%)
  matrix products  55.9 us (8%)
  between operations  15.4 us (2%)
    all_gather x1, waiting for transfers between devices, body(): w_piece = jnp.concatenate(all_gather(fixed_down_weight, 'dp'), axis=1)  296 us
    unnamed x2, blocking collectives  122 us
    reduce_scatter x1, waiting for transfers between devices, body(): lax.psum_scatter(products, 'tensor', scatter_dimension=1, tiled=True)  70.4 us
    unnamed x41, local copies, waits for them, and re-layouts  64.5 us
    reshape x1, local copies, waits for them, and re-layouts, body(): w_piece = jnp.concatenate(all_gather(fixed_down_weight, 'dp'), axis=1)  56.8 us
    dot_general x1, matrix products, body(): products = jnp.dot(hidden, w_piece, preferred_element_type=jnp.float32)  37.5 us
    all_gather x1, blocking collectives, body(): factor_a_slice = lax.all_gather(lowrank_factor_a, 'dp', axis=1, tiled=True)  24.5 us
  transfers between devices with their start and end apart: 4, of which 2 were waited for; matrix products, arithmetic and copies ran while one was open for 24% of the time, Pallas kernels for 0%

profile of v1, /device:TPU:0, one launch (start us, length us, event | category | flops | bytes accessed | tf_op | source)
XLA Modules:
  0.0 720.9 jit_solution(7452878573167720599)
XLA Ops:
  7.2 0.7 all-gather.4.cloned.1.call-update
  8.0 24.5 %all-gather.1 = bf16[16,288,16]{1,2,0:T(8,128)(2,1)S(1)} all-gather(bf16[1,288,16]{1,2,0:T(8,128)(2,1)S(1)} %bitcast.33), channel_id=1, replica_groups=mesh['dp'=16,'tensor'=2] {'dp'}, dimensions={0}, use_global_device_ids=true | all-gather | bytes 156672 | tf_op jit(solution)/shard_map/all_gather | solution.py:23
  32.8 0.6 fusion.17
  34.1 4.4 fusion.3
  38.4 4.9 psum.22
  43.4 0.2 dynamic-update-slice
  43.6 61.0 %all-reduce = f32[4608]{0:T(1024)S(1)} all-reduce(f32[4608]{0:T(1024)S(1)} %dynamic-update-slice), channel_id=1, replica_groups=mesh['dp'=16,'tensor'=2] {'dp'}, use_global_device_ids=true, to_apply=%add | all-reduce | flops 4608 | bytes 36864
  104.8 0.5 fusion.4
  105.3 4.3 fusion.19
  109.6 8.7 %all-reduce.2 = (bf16[320,16]{0,1:T(8,128)(2,1)S(1)}, bf16[320,16]{0,1:T(8,128)(2,1)S(1)}) all-reduce(f32[320,16]{0,1:T(8,128)S(1)} %fusion.19, f32[320,16]{0,1:T(8,128)S(1)} %fusion.4), channel_id=1, replica_groups=mesh['dp'=16,'tensor'=2] {'tensor'}, use_global_device_ids=true, to_apply=%region_1.0 | all-reduce | flops 10240 | bytes 61440 | tf_op jit(solution)/shard_map/psum | solution.py:16
  118.3 1.8 convolution_bitcast_fusion.1
  120.2 3.7 convolution_bitcast_fusion
  124.0 2.9 copy.17
  126.9 0.2 reduce-scatter.8.cloned.1.call-start
  127.1 296.4 %all-gather.4.cloned.1.call-done = bf16[147456,288]{0,1:T(8,128)(2,1)} async-done(((bf16[9216,288]{0,1:T(8,128)(2,1)}), bf16[147456,288]{0,1:T(8,128)(2,1)}) %all-gather.4.cloned.1.call-update) | async-done | bytes 84934672 | tf_op jit(solution)/shard_map/all_gather | solution.py:22
  423.5 56.5 %copy.19 = bf16[36,8,16,9216]{3,2,1,0:T(8,128)(2,1)} copy(bf16[36,8,16,9216]{3,1,2,0:T(8,128)(2,1)} %bitcast.12) | data formatting | bytes 169869312
  480.1 56.8 %copy.13 = bf16[9216,16,288]{0,2,1:T(8,128)(2,1)} copy(bf16[9216,16,288]{0,1,2:T(8,128)(2,1)} %bitcast) | data formatting | bytes 169869312 | tf_op jit(solution)/shard_map/reshape | solution.py:22
  536.8 37.5 %fusion.18 = f32[320,4608]{1,0:T(8,128)} fusion(bf16[320,9216]{1,0:T(8,128)(2,1)S(1)} %bitcast.31, bf16[9216,4608]{0,1:T(8,128)(2,1)} %bitcast.1), kind=kOutput, calls=%fused_computation.24 | convolution fusion | flops 27179089920 | bytes 96731136 | tf_op jit(solution)/shard_map/dot_general | solution.py:24
  575.1 1.6 copy.16
  576.7 1.7 copy.18
  578.4 70.4 %reduce-scatter.8.cloned.1.call-done = f32[320,2304]{1,0:T(8,128)} async-done(((f32[320,4608]{1,0:T(8,128)}), f32[320,2304]{1,0:T(8,128)}) %reduce-scatter.8.cloned.1.call-update) | async-done | bytes 2949136 | tf_op jit(solution)/shard_map/reduce_scatter | solution.py:31
  648.9 3.7 fusion.1
  652.6 61.1 %all-reduce.1 = f32[2304]{0:T(1024)S(1)} all-reduce(f32[2304]{0:T(1024)S(1)} %fusion.12), channel_id=4, replica_groups=mesh['dp'=16,'tensor'=2] {'dp'}, use_global_device_ids=true, to_apply=%region_5.0.clone | all-reduce | flops 2304 | bytes 18432
  713.7 0.6 dynamic-slice.3
  (46 shorter events, 0.7 us)
Async XLA Ops:
  7.2 26.9 %copy-start = (bf16[9216,16]{0,1:T(8,128)(2,1)S(1)}, bf16[9216,16]{0,1:T(8,128)(2,1)}, u32[]{:S(2)}) copy-start(bf16[9216,16]{0,1:T(8,128)(2,1)} %param.8) | copy-start | bytes 884740
  7.2 25.6 %copy-start.13 = (u32[32]{0:T(128)S(1)}, u32[32]{0:T(128)}, u32[]{:S(2)}) copy-start(u32[32]{0:T(128)} %constant.16) | copy-start | bytes 388
  7.2 0.8 copy-start.11
  7.2 416.3 %all-gather.4.cloned.1.call-start = ((), (), s32[]{:S(2)}) async-start(), calls=%async_computation.4 | async-start | bytes 90243072 | tf_op jit(solution)/shard_map/all_gather | solution.py:22
  7.9 567.2 %reduce-scatter.10.cloned.1.call-start = ((), (), s32[]{:S(2)}) async-start(), calls=%async_computation.5 | async-start | bytes 1253376
  32.8 72.0 %copy-start.3 = (bf16[4608,16]{0,1:T(8,128)(2,1)}, bf16[4608,16]{0,1:T(8,128)(2,1)S(1)}, u32[]{:S(2)}) copy-start(bf16[4608,16]{0,1:T(8,128)(2,1)S(1)} %reshape.22) | copy-start | bytes 442372
  34.0 70.6 %copy-start.12 = (f32[2304]{0:T(1024)S(1)}, f32[2304]{0:T(1024)}, u32[]{:S(2)}) copy-start(f32[2304]{0:T(1024)} %param.10) | copy-start | bytes 27652
  34.1 70.7 %copy-start.1 = (bf16[320,2304]{1,0:T(8,128)(2,1)S(1)}, bf16[320,2304]{1,0:T(8,128)(2,1)}, u32[]{:S(2)}) copy-start(bf16[320,2304]{1,0:T(8,128)(2,1)} %param.11) | copy-start | bytes 4423684
  104.6 5.0 copy-start.7
  104.8 13.6 %copy-start.5 = (f32[2304]{0:T(1024)}, f32[2304]{0:T(1024)S(1)}, u32[]{:S(2)}) copy-start(f32[2304]{0:T(1024)S(1)} %fusion.11) | copy-start | bytes 27652
  118.3 1.9 copy-start.9
  120.2 456.5 %reduce-scatter.12.cloned.1.call-start = ((), (), s32[]{:S(2)}) async-start(), calls=%async_computation.6 | async-start | bytes 5013504
  126.9 522.0 %reduce-scatter.8.cloned.1.call-start = ((), (), s32[]{:S(2)}) async-start(), calls=%async_computation.3 | async-start | bytes 8847360 | tf_op jit(solution)/shard_map/reduce_scatter | solution.py:31
  423.5 113.3 %slice-start = ((s8[5898240]{0:T(1024)(128)(4,1)}), s8[4194304]{0:T(1024)(128)(4,1)S(1)}, s32[]{:S(2)}) async-start(s8[5898240]{0:T(1024)(128)(4,1)} %bitcast.30), calls=%async_computation.7 | async-start | bytes 8388608
  480.1 56.8 %slice-start.1 = ((s8[5898240]{0:T(1024)(128)(4,1)}), s8[1703936]{0:T(1024)(128)(4,1)S(1)}, s32[]{:S(2)}) async-start(s8[5898240]{0:T(1024)(128)(4,1)} %bitcast.30), calls=%async_computation.8 | async-start | bytes 3407872
  574.3 74.5 %copy-start.2 = (bf16[320,2304]{1,0:T(8,128)(2,1)S(1)}, bf16[320,2304]{1,0:T(8,128)(2,1)}, u32[]{:S(2)}) copy-start(bf16[320,2304]{1,0:T(8,128)(2,1)} %param.11) | copy-start | bytes 4423684
  574.3 74.5 %copy-start.4 = (bf16[4608,16]{0,1:T(8,128)(2,1)S(1)}, bf16[4608,16]{0,1:T(8,128)(2,1)}, u32[]{:S(2)}) copy-start(bf16[4608,16]{0,1:T(8,128)(2,1)} %copy-done.3) | copy-start | bytes 442372
  574.3 74.5 %copy-start.6 = (f32[2304]{0:T(1024)S(1)}, f32[2304]{0:T(1024)}, u32[]{:S(2)}) copy-start(f32[2304]{0:T(1024)} %copy-done.5) | copy-start | bytes 27652
  574.3 74.5 %copy-start.10 = (bf16[320,16]{0,1:T(8,128)(2,1)S(1)}, bf16[320,16]{0,1:T(8,128)(2,1)}, u32[]{:S(2)}) copy-start(bf16[320,16]{0,1:T(8,128)(2,1)} %copy-done.9) | copy-start | bytes 30724
  578.4 74.1 %copy-start.8 = (f32[4608]{0:T(1024)S(1)}, f32[4608]{0:T(1024)}, u32[]{:S(2)}) copy-start(f32[4608]{0:T(1024)} %copy-done.7) | copy-start | bytes 55300
Sparse Core Ops, SparseCore 0:
  9.6 413.9 all-gather.3
  427.7 58.9 reduce-scatter.9
  490.5 74.6 reduce-scatter.11
  574.5 74.3 reduce-scatter.7
